TPU v7x, 256 devices: a whole 4x4x8 slice. The times are simulated.
256 devices in a mesh: wide: 64 (over z, y, core), narrow: 4 (over x).
Axes of the slice: x: 4, y: 4, z: 8, core: 2. Of those that a mesh axis runs over, the one named last changes fastest.
Arguments:
- coords_inner: float32 [2, 65536], P(None, ('wide', 'narrow')), may hold values from -1 to 1
- velocity: float32 [2, 65536], P(None, ('wide', 'narrow')), may hold values from -6 to 6
- source: float32 [65536], P(('wide', 'narrow')), may hold values from -6 to 6
- coords_edge: float32 [2, 32768], P(None, ('wide', 'narrow')), may hold values from -1 to 1
- flux_weight: float32 [2, 32768], P(None, ('wide', 'narrow')), may hold values from -6 to 6
- owner: int32 [32768, 1], P(('wide', 'narrow')), may hold values from 0 to 63; in each aligned block of 128 rows (0 to 127, 128 to 255, ...) at most 4 rows name the same one
- local_face: int32 [32768], P(('wide', 'narrow')), may hold values from 0 to 127
- w_first: float32 [2, 512], replicated, may hold values from -4 to 4
- b_first: float32 [512], replicated, may hold values from -3 to 3
- w_hidden: float32 [4, 512, 512], replicated, may hold values from -0.25 to 0.25
- b_hidden: float32 [4, 512], replicated, may hold values from -3 to 3
- w_last: float32 [512], replicated, may hold values from -0.25 to 0.25
Outputs:
- face_integral: float32 [8192], P('wide')
- grad_first: float32 [2, 512], replicated
- grad_hidden: float32 [4, 512, 512], replicated
- grad_last: float32 [512], replicated
Inputs may be any that keep to these rules, and one draw needn't show every extreme that they name: Among the 128 face points of one device no owner appears more than 4 times, and some owner appears exactly 4 times.
All inputs are finite; a program needn't handle non-finite values.
Results may differ from a plain program's by a relative error of at most 0.0003.
Values sent between devices are 32-bit elements; how exact they have to be, the bound alone decides.
A program may use at most 128 MiB of HBM per device.

v0:
```python
import math
import jax
import jax.numpy as jnp
from jax import lax
from jax.sharding import PartitionSpec as P

FACE_DEV = 128
penalty_weight = 4.0
BOTH = ("wide", "narrow")
precise = lax.Precision.HIGH


def forward(coords, direction, w_first, b_first, w_hidden, b_hidden, w_last):
    hidden = jnp.tanh(
        coords[0][:, None] * w_first[0][None] + coords[1][:, None] * w_first[1][None] + b_first
    )
    tangent = (1.0 - hidden * hidden) * (
        direction[0][:, None] * w_first[0][None] + direction[1][:, None] * w_first[1][None]
    )
    points = hidden.shape[0]
    kept = [(hidden, None, tangent)]
    for level in range(w_hidden.shape[0]):
        product = jnp.dot(jnp.concatenate([hidden, tangent], 0), w_hidden[level], precision=precise)
        hidden = jnp.tanh(product[:points] + b_hidden[level])
        slope = product[points:]
        tangent = (1.0 - hidden * hidden) * slope
        kept.append((hidden, slope, tangent))
    value = jnp.sum(hidden * w_last[None], 1)
    slopes = jnp.sum(tangent * w_last[None], 1)
    return (value, slopes, kept)


def backward(coords, direction, kept, hidden_cot, tangent_cot, w_first, w_hidden):
    grads = []
    for level in reversed(range(w_hidden.shape[0])):
        hidden, slope, _ = kept[level + 1]
        gate = 1.0 - hidden * hidden
        product_cot = gate * tangent_cot
        sum_cot = gate * (hidden_cot - 2.0 * hidden * slope * tangent_cot)
        cots = jnp.concatenate([sum_cot, product_cot], 0)
        below = jnp.concatenate([kept[level][0], kept[level][2]], 0)
        grads.append(lax.dot_general(below, cots, (((0,), (0,)), ((), ())), precision=precise))
        down = lax.dot_general(cots, w_hidden[level], (((1,), (1,)), ((), ())), precision=precise)
        points = hidden.shape[0]
        hidden_cot, tangent_cot = (down[:points], down[points:])
    hidden, _, _ = kept[0]
    gate = 1.0 - hidden * hidden
    start = direction[0][:, None] * w_first[0][None] + direction[1][:, None] * w_first[1][None]
    start_cot = gate * tangent_cot
    sum_cot = gate * (hidden_cot - 2.0 * hidden * start * tangent_cot)
    first = jnp.stack(
        [
            jnp.sum(coords[j][:, None] * sum_cot + direction[j][:, None] * start_cot, 0)
            for j in range(2)
        ]
    )
    return (first, jnp.stack(grads[::-1], 0))


def local(
    coords_inner,
    velocity,
    source,
    coords_edge,
    flux_weight,
    owner,
    local_face,
    w_first,
    b_first,
    w_hidden,
    b_hidden,
    w_last,
):
    devices = lax.axis_size(BOTH)
    inner_rows = coords_inner.shape[1]
    edge_rows = coords_edge.shape[1]
    inner_scale = 2.0 / math.sqrt(inner_rows * devices)
    face_scale = 2.0 * penalty_weight / math.sqrt(FACE_DEV * lax.axis_size("wide"))
    net = (w_first, b_first, w_hidden, b_hidden, w_last)
    _, flux, kept_edge = forward(coords_edge, flux_weight, *net)
    face = owner[:, 0] * FACE_DEV + local_face
    mine = jnp.stack([flux, face.astype(jnp.float32)], 0)
    everyone = lax.all_gather(mine, BOTH)
    all_flux = everyone[:, 0].reshape(-1)
    all_face = everyone[:, 1].reshape(-1)

    def sums(wanted):
        return jnp.sum(
            jnp.where(wanted.astype(jnp.float32)[:, None] == all_face[None], all_flux[None], 0.0), 1
        )

    reached = sums(face)
    integral = sums(lax.axis_index("wide") * FACE_DEV + jnp.arange(FACE_DEV))
    value, slopes, kept_inner = forward(coords_inner, velocity, *net)
    inner_cot = inner_scale * (slopes + value - source)
    edge_cot = face_scale * reached
    coords = jnp.concatenate([coords_inner, coords_edge], 1)
    direction = jnp.concatenate([velocity, flux_weight], 1)
    kept = [
        tuple((None if a is None else jnp.concatenate([a, b], 0) for a, b in zip(one, two)))
        for one, two in zip(kept_inner, kept_edge)
    ]
    hidden_out = jnp.concatenate([inner_cot, jnp.zeros_like(edge_cot)])[:, None]
    tangent_out = jnp.concatenate([inner_cot, edge_cot])[:, None]
    last = jnp.sum(hidden_out * kept[-1][0] + tangent_out * kept[-1][2], 0)
    first, hidden = backward(
        coords,
        direction,
        kept,
        hidden_out * w_last[None],
        tangent_out * w_last[None],
        w_first,
        w_hidden,
    )
    first, hidden, last = lax.psum((first, hidden, last), BOTH)
    return (integral, first, hidden, last)


def solution(mesh):
    points = P(None, BOTH)
    in_specs = (
        points,
        points,
        P(BOTH),
        points,
        points,
        P(BOTH, None),
        P(BOTH),
        P(),
        P(),
        P(),
        P(),
        P(),
    )
    out_specs = (P("wide"), P(), P(), P())
    return jax.shard_map(local, mesh=mesh, in_specs=in_specs, out_specs=out_specs, check_vma=False)
```

profile of v0, /device:TPU:2, one launch (start us, length us, event | category | flops | bytes accessed | tf_op | source)
XLA Modules:
  0.0 388.6 jit_solution(4115349576246029402)
XLA Ops:
  7.2 0.0 all-reduce.4.cloned.1.call-start
  7.2 0.8 fusion.155
  8.0 0.8 fusion.156
  8.7 0.8 fusion.154
  9.5 0.9 fusion.153
  10.4 0.8 slice_bitcast_fusion.1
  11.1 0.8 add_tanh_fusion.1
  12.0 1.8 fusion.78
  13.8 0.1 subtract_multiply_fusion.7
  13.9 2.0 fusion.74
  15.9 0.1 subtract_multiply_fusion.6
  16.0 0.3 copy-done
  16.3 0.7 fusion.70
  17.0 0.1 subtract_multiply_fusion.5
  17.1 0.6 fusion.66
  17.8 0.2 multiply_reduce_fusion.2
  18.0 67.6 %all-gather.1 = f32[256,2,128]{2,1,0:T(2,128)S(1)} all-gather(f32[1,2,128]{2,1,0:T(2,128)S(1)} %maximum_bitcast_fusion), channel_id=2, replica_groups=mesh['wide'=64,'narrow'=4] {'wide','narrow'}, dimensions={0}, use_global_device_ids=true | all-gather | bytes 263168 | tf_op jit(solution)/shard_map/all_gather | solution.py:83
  85.6 0.2 fusion.152
  85.8 4.7 %select_reduce_fusion = (f32[128]{0:T(128)S(1)}, f32[128]{0:T(128)}) fusion(f32[32768]{0:T(1024)S(1)} %bitcast.67, f32[32768]{0:T(1024)S(1)} %bitcast.66, f32[128]{0:T(128)S(1)} %get-tuple-element.74, f32[128]{0:T(128)S(1)} %get-tuple-element.75), kind=kLoop, calls=%fused_computation | loop fusion | flops 25165568 | bytes 264192 | tf_op jit(solution)/shard_map/reduce_sum | solution.py:88
  90.5 0.3 add_tanh_fusion
  90.8 1.0 fusion.48
  91.8 0.2 subtract_multiply_fusion.3
  92.0 1.1 fusion.52
  93.0 0.2 subtract_multiply_fusion.2
  93.2 1.0 fusion.56
  94.3 0.2 subtract_multiply_fusion.1
  94.5 1.1 fusion.60
  95.5 0.2 multiply_reduce_fusion
  95.8 0.4 copy-done.7
  96.2 0.4 fusion.102
  96.6 1.5 fusion.32
  98.2 1.7 fusion.47
  99.9 0.4 fusion.97
  100.3 1.5 fusion.35
  101.8 1.5 fusion.46
  103.3 0.4 fusion.96
  103.7 1.5 fusion.38
  105.2 1.5 fusion.45
  106.6 0.4 fusion.95
  107.0 1.5 fusion.41
  108.5 2.5 pad_maximum_fusion
  111.0 0.0 all-reduce.4.cloned.1.call-update
  111.0 0.6 copy-done.3
  111.7 2.7 fusion.44
  114.4 0.6 add_reduce_fusion.1
  115.0 73.2 %all-reduce.1 = (f32[2,512]{1,0:T(2,128)}, f32[512]{0:T(512)}) all-reduce(f32[2,512]{1,0:T(2,128)S(1)} %pad_maximum_fusion.18, f32[512]{0:T(512)S(1)} %get-tuple-element.43), channel_id=1, replica_groups=mesh['wide'=64,'narrow'=4] {'wide','narrow'}, use_global_device_ids=true, to_apply=%region_7.8 | all-reduce | flops 1536 | bytes 12288 | tf_op jit(solution)/shard_map/psum | solution.py:115
  188.3 188.8 %all-reduce.4.cloned.1.call-done = f32[4,512,512]{2,1,0:T(8,128)} async-done(((f32[4,512,512]{2,1,0:T(8,128)}), f32[4,512,512]{2,1,0:T(8,128)}) %all-reduce.4.cloned.1.call-update) | async-done | bytes 4194320 | tf_op jit(solution)/shard_map/psum | solution.py:115
  377.1 4.6 %copy.19 = f32[4,512,512]{2,1,0:T(8,128)} copy(f32[4,512,512]{2,1,0:T(8,128)} %all-reduce.4.cloned.1.call-done) | data formatting | bytes 8388608
  (28 shorter events, 0.2 us)
Async XLA Ops:
  7.2 369.9 %all-reduce.4.cloned.1.call-start = ((), (), s32[]{:S(2)}) async-start(), calls=%async_computation | async-start | bytes 8388608 | tf_op jit(solution)/shard_map/psum | solution.py:115
  13.8 2.5 copy-start
  17.0 0.8 copy-start.8
  17.0 0.8 copy-start.9
  17.0 0.8 copy-start.1
  17.8 72.7 %copy-start.2 = (f32[512]{0:T(512)S(1)}, f32[512]{0:T(512)}, u32[]{:S(2)}) copy-start(f32[512]{0:T(512)} %param.20) | copy-start | bytes 6148
  95.5 0.7 copy-start.7
  111.0 0.7 copy-start.3
  111.0 0.7 copy-start.5
  111.0 0.7 copy-start.4
  111.0 0.7 copy-start.6
Sparse Core Ops, SparseCore 0:
  111.1 265.9 all-reduce.3
where the time goes:
time: 389 us
  waiting for transfers between devices  189 us (49%)
  blocking collectives  141 us (36%)
  matrix products  22.6 us (6%)
  between operations  14.4 us (4%)
  other arithmetic  11.6 us (3%)
  local copies, waits for them, and re-layouts  10.3 us (3%)
    psum x1, waiting for transfers between devices, local(): first, hidden, last = lax.psum((first, hidden, last), BOTH)  189 us
    psum x1, blocking collectives, local(): first, hidden, last = lax.psum((first, hidden, last), BOTH)  73.2 us
    all_gather x1, blocking collectives, local(): everyone = lax.all_gather(mine, BOTH)  67.6 us
    dot_general x8, matrix products, forward(): jnp.dot(jnp.concatenate([hidden, tangent], 0), w_hidden[level], precision...  9.35 us
  transfers between devices with their start and end apart: 1, of which 1 were waited for; matrix products, arithmetic and copies ran while one was open for 1% of the time, Pallas kernels for 0%

commit v1 on v0

--- a/solution.py
+++ b/solution.py
@@ -112,7 +112,7 @@
         w_first,
         w_hidden,
     )
-    first, hidden, last = lax.psum((first, hidden, last), BOTH)
+    first, hidden, last = lax.psum(lax.psum((first, hidden, last), "wide"), "narrow")
     return (integral, first, hidden, last)
 
 

time: 389 us -> 458 us (1.18)
  blocking collectives: 141 us -> 206 us
    psum x1 -> x2, blocking collectives: 73.2 us -> 139 us  [the longest x1 130 us: local(): lax.psum((first, hidden, last), 'wide')]
    psum x1 -> x2, waiting for transfers between devices: 189 us -> 192 us  [the longest x1 192 us: local(): lax.psum((first, hidden, last), 'wide')]
  transfers between devices with their start and end apart: 1 -> 2, of which waited for: 1 -> 1; matrix products, arithmetic and copies ran while one was open for 1% -> 1% of each run, Pallas kernels for 0% -> 0%
where the time goes in v1:
time: 458 us; the launch traced here: 457 us
  blocking collectives  206 us (45%)
  waiting for transfers between devices  192 us (42%)
  matrix products  22.6 us (5%)
  between operations  14.4 us (3%)
  other arithmetic  11.6 us (3%)
  local copies, waits for them, and re-layouts  10.3 us (2%)
    psum x1, waiting for transfers between devices, local(): lax.psum((first, hidden, last), 'wide')  192 us
    psum x1, blocking collectives, local(): lax.psum((first, hidden, last), 'wide')  130 us
    all_gather x1, blocking collectives, local(): everyone = lax.all_gather(mine, BOTH)  67.6 us
    dot_general x8, matrix products, forward(): jnp.dot(jnp.concatenate([hidden, tangent], 0), w_hidden[level], precision...  9.35 us
    psum x1, blocking collectives, local(): lax.psum(lax.psum((first, hidden, last), 'wide'), 'narrow')  9.27 us
  transfers between devices with their start and end apart: 2, of which 1 were waited for; matrix products, arithmetic and copies ran while one was open for 1% of the time, Pallas kernels for 0%

profile of v1, /device:TPU:2, one launch (start us, length us, event | category | flops | bytes accessed | tf_op | source)
XLA Modules:
  0.0 457.4 jit_solution(1836947949143250377)
XLA Ops:
  7.2 0.8 fusion.155
  8.0 0.8 fusion.156
  8.7 0.8 fusion.154
  9.5 0.9 fusion.153
  10.4 0.8 slice_bitcast_fusion.1
  11.2 0.8 add_tanh_fusion.1
  12.0 1.8 fusion.78
  13.9 0.1 subtract_multiply_fusion.7
  13.9 2.0 fusion.74
  16.0 0.1 subtract_multiply_fusion.6
  16.0 0.3 copy-done
  16.4 0.7 fusion.70
  17.1 0.1 subtract_multiply_fusion.5
  17.1 0.6 fusion.66
  17.8 0.2 multiply_reduce_fusion.2
  18.0 67.6 %all-gather.1 = f32[256,2,128]{2,1,0:T(2,128)S(1)} all-gather(f32[1,2,128]{2,1,0:T(2,128)S(1)} %maximum_bitcast_fusion), channel_id=2, replica_groups=mesh['wide'=64,'narrow'=4] {'wide','narrow'}, dimensions={0}, use_global_device_ids=true | all-gather | bytes 263168 | tf_op jit(solution)/shard_map/all_gather | solution.py:83
  85.6 0.2 fusion.152
  85.8 4.7 %select_reduce_fusion = (f32[128]{0:T(128)S(1)}, f32[128]{0:T(128)}) fusion(f32[32768]{0:T(1024)S(1)} %bitcast.67, f32[32768]{0:T(1024)S(1)} %bitcast.66, f32[128]{0:T(128)S(1)} %get-tuple-element.76, f32[128]{0:T(128)S(1)} %get-tuple-element.77), kind=kLoop, calls=%fused_computation | loop fusion | flops 25165568 | bytes 264192 | tf_op jit(solution)/shard_map/reduce_sum | solution.py:88
  90.5 0.3 add_tanh_fusion
  90.8 1.0 fusion.48
  91.8 0.2 subtract_multiply_fusion.3
  92.0 1.1 fusion.52
  93.1 0.2 subtract_multiply_fusion.2
  93.2 1.1 fusion.56
  94.3 0.2 subtract_multiply_fusion.1
  94.5 1.0 fusion.60
  95.5 0.2 multiply_reduce_fusion
  95.8 0.4 copy-done.7
  96.2 0.4 fusion.102
  96.7 1.5 fusion.32
  98.2 1.7 fusion.47
  99.9 0.4 fusion.97
  100.3 1.5 fusion.35
  101.8 1.5 fusion.46
  103.3 0.4 fusion.96
  103.7 1.5 fusion.38
  105.2 1.5 fusion.45
  106.6 0.4 fusion.95
  107.0 1.5 fusion.41
  108.5 2.5 pad_maximum_fusion
  111.0 0.0 all-reduce.8.cloned.1.call-start
  111.1 191.9 %all-reduce.6.cloned.1.call-done = f32[4,512,512]{2,1,0:T(8,128)} async-done(((f32[4,512,512]{2,1,0:T(8,128)}), f32[4,512,512]{2,1,0:T(8,128)}) %all-reduce.6.cloned.1.call-update) | async-done | bytes 4194320 | tf_op jit(solution)/shard_map/psum | solution.py:115
  303.0 0.6 copy-done.3
  303.7 2.7 fusion.44
  306.4 0.6 add_reduce_fusion.1
  307.0 129.6 %all-reduce.1 = (f32[2,512]{1,0:T(2,128)S(1)}, f32[512]{0:T(512)S(1)}) all-reduce(f32[2,512]{1,0:T(2,128)S(1)} %pad_maximum_fusion.18, f32[512]{0:T(512)S(1)} %get-tuple-element.45), channel_id=1, replica_groups=mesh['wide'=64,'narrow'=4] {'wide'}, use_global_device_ids=true, to_apply=%region_7.8 | all-reduce | flops 1536 | bytes 12288 | tf_op jit(solution)/shard_map/psum | solution.py:115
  436.7 9.3 %all-reduce.2 = (f32[2,512]{1,0:T(2,128)}, f32[512]{0:T(512)}) all-reduce(f32[2,512]{1,0:T(2,128)S(1)} %get-tuple-element.14, f32[512]{0:T(512)S(1)} %get-tuple-element.15), channel_id=1, replica_groups=mesh['wide'=64,'narrow'=4] {'narrow'}, use_global_device_ids=true, to_apply=%region_8.9 | all-reduce | flops 1536 | bytes 12288 | tf_op jit(solution)/shard_map/psum | solution.py:115
  445.9 4.6 %copy.20 = f32[4,512,512]{2,1,0:T(8,128)} copy(f32[4,512,512]{2,1,0:T(8,128)} %all-reduce.8.cloned.1.call-done) | data formatting | bytes 8388608
  (32 shorter events, 0.2 us)
Async XLA Ops:
  7.2 295.8 %all-reduce.6.cloned.1.call-start = ((), (), s32[]{:S(2)}) async-start(), calls=%async_computation | async-start | bytes 8388608 | tf_op jit(solution)/shard_map/psum | solution.py:115
  13.9 2.5 copy-start
  17.0 0.8 copy-start.8
  17.0 0.8 copy-start.9
  17.0 0.8 copy-start.1
  17.8 72.7 %copy-start.2 = (f32[512]{0:T(512)S(1)}, f32[512]{0:T(512)}, u32[]{:S(2)}) copy-start(f32[512]{0:T(512)} %param.20) | copy-start | bytes 6148
  95.5 0.7 copy-start.7
  111.0 334.9 %all-reduce.8.cloned.1.call-start = ((), (), s32[]{:S(2)}) async-start(), calls=%async_computation.1 | async-start | bytes 8388608 | tf_op jit(solution)/shard_map/psum | solution.py:115
  303.0 0.7 copy-start.3
  303.0 0.7 copy-start.5
  303.0 0.7 copy-start.4
  303.0 0.7 copy-start.6
Sparse Core Ops, SparseCore 0:
  111.1 191.8 all-reduce.5
  305.3 95.5 all-reduce.7
